TPU v7x, 32 devices: a whole 2x2x4 slice. The times are simulated.
32 devices in a mesh: smp: 8 (over z, y), var: 4 (over x, core).
Axes of the slice: x: 2, y: 2, z: 4, core: 2. Of those that a mesh axis runs over, the one named last changes fastest.
Arguments:
- dosage: int32 [512, 2048], P('smp', 'var'), may hold values from -2147483648 to 2147483647, as said below
- shares_init: float32 [12, 8192], P(None, ('smp', 'var')), may hold values from 0.1 to 1
- freqs_init: float32 [12, 2048], P(None, ('var', 'smp')), may hold values from 0.019 to 0.981
Outputs:
- shares: float32 [12, 8192], P(None, ('smp', 'var'))
- freqs: float32 [12, 2048], P(None, ('var', 'smp'))
Inputs may be any that keep to these rules, and one draw needn't show every extreme that they name: Every 2-bit code in a word of dosage is 0, 1, 2 or 3, and 3 marks a missing genotype.
All inputs are finite; a program needn't handle non-finite values.
Results may differ from a plain program's by a relative error of at most 0.0003.
Values sent between devices are 32-bit elements; how exact they have to be, the bound alone decides.
A program may use at most 64 MiB of HBM per device.

v0:
```python
import jax
import jax.numpy as jnp
from jax import lax
from jax.sharding import PartitionSpec as P

ITERS = 2


HIGH = lax.Precision.HIGHEST


def unpack_codes(packed):
    shifts = 2 * jnp.arange(16, dtype=jnp.int32)
    codes = jnp.bitwise_and(jnp.right_shift(packed[:, None, :], shifts[None, :, None]), 3)
    return codes.reshape(packed.shape[0] * 16, packed.shape[1])


def expect_sums(packed, shares_block, freqs_block):
    codes = unpack_codes(packed)
    live = (codes < 3).astype(jnp.float32)
    allele_f = live * codes.astype(jnp.float32)
    probs = jnp.einsum("kn,km->nm", shares_block, freqs_block, precision=HIGH)
    ratio_alt = allele_f / probs
    ratio_ref = (2.0 * live - allele_f) / (1.0 - probs)
    sum_q = jnp.einsum("km,nm->kn", freqs_block, ratio_alt, precision=HIGH) + jnp.einsum(
        "km,nm->kn", 1.0 - freqs_block, ratio_ref, precision=HIGH
    )
    sum_a = jnp.einsum("kn,nm->km", shares_block, ratio_alt, precision=HIGH)
    sum_b = jnp.einsum("kn,nm->km", shares_block, ratio_ref, precision=HIGH)
    return (sum_q, sum_a, sum_b)


def block_sums(packed, shares_block, freqs_block):
    word_rows = min(packed.shape[0], 16)
    blocks = packed.shape[0] // word_rows
    populations = shares_block.shape[0]
    packed_blocks = packed.reshape(blocks, word_rows, packed.shape[1])
    share_blocks = shares_block.reshape(populations, blocks, word_rows * 16).transpose(1, 0, 2)

    def one_block(carry, items):
        sum_q, sum_a, sum_b = expect_sums(items[0], items[1], freqs_block)
        return ((carry[0] + sum_a, carry[1] + sum_b), sum_q)

    start = (jnp.zeros(freqs_block.shape, jnp.float32), jnp.zeros(freqs_block.shape, jnp.float32))
    totals, sums_q = lax.scan(one_block, start, (packed_blocks, share_blocks))
    sum_q = sums_q.transpose(1, 0, 2).reshape(populations, shares_block.shape[1])
    return (sum_q, totals[0], totals[1])


def renew_shares(shares_block, sum_q):
    numer = shares_block * sum_q
    return (numer + 0.5) / (jnp.sum(numer, axis=0, keepdims=True) + 0.5 * shares_block.shape[0])


def renew_freqs(freqs_block, sum_a, sum_b):
    alt_part = freqs_block * sum_a
    ref_part = (1.0 - freqs_block) * sum_b
    return (alt_part + 0.5) / (alt_part + ref_part + 1.0)


def body(dosage, shares_init, freqs_init):
    own_shares = shares_init / jnp.sum(shares_init, axis=0, keepdims=True)
    own_freqs = freqs_init
    share_width = shares_init.shape[1]
    freq_width = freqs_init.shape[1]
    shares_block = lax.all_gather(own_shares, "var", axis=1, tiled=True)
    freqs_block = lax.all_gather(own_freqs, "smp", axis=1, tiled=True)
    for iteration in range(ITERS):
        part_q, part_a, part_b = block_sums(dosage, shares_block, freqs_block)
        sum_q = lax.psum(part_q, "var")
        sum_a, sum_b = lax.psum((part_a, part_b), "smp")
        shares_block = renew_shares(shares_block, sum_q)
        freqs_block = renew_freqs(freqs_block, sum_a, sum_b)
        if iteration + 1 == ITERS:
            own_shares = lax.dynamic_slice_in_dim(
                shares_block, lax.axis_index("var") * share_width, share_width, 1
            )
            own_freqs = lax.dynamic_slice_in_dim(
                freqs_block, lax.axis_index("smp") * freq_width, freq_width, 1
            )
    return (own_shares, own_freqs)


def solution(mesh):
    placed = (P("smp", "var"), P(None, ("smp", "var")), P(None, ("var", "smp")))
    return jax.shard_map(
        body,
        mesh=mesh,
        in_specs=placed,
        out_specs=(P(None, ("smp", "var")), P(None, ("var", "smp"))),
        check_vma=False,
    )
```

profile of v0, /device:TPU:0, one launch (start us, length us, event | category | flops | bytes accessed | tf_op | source)
XLA Modules:
  0.0 156.3 jit_solution(4070201371241163746)
XLA Ops:
  0.6 0.8 reduce_sum.27
  1.4 6.2 %all_gather.6 = f32[12,1024]{1,0:T(8,128)S(1)} all-gather(f32[12,256]{1,0:T(8,128)S(1)} %broadcast_divide_fusion), channel_id=1, replica_groups=mesh['smp'=8,'var'=4] {'var'}, dimensions={1}, use_global_device_ids=true | all-gather | bytes 61440 | tf_op jit(solution)/shard_map/all_gather | solution.py:66
  7.7 0.7 copy-done.2
  8.4 31.4 %all-gather = f32[8,64,12]{1,2,0:T(8,128)S(1)} all-gather(f32[1,64,12]{1,2,0:T(8,128)S(1)} %bitcast.171), channel_id=1, replica_groups=mesh['smp'=8,'var'=4] {'smp'}, dimensions={0}, use_global_device_ids=true | all-gather | bytes 27648 | tf_op jit(solution)/shard_map/all_gather | solution.py:67
  39.9 0.8 copy-done
  40.7 10.8 %while.30 = (s32[]{:T(128)}, f32[12,512]{1,0:T(8,128)S(1)}, f32[12,512]{1,0:T(8,128)S(1)}, f32[4,12,256]{2,1,0:T(8,128)S(1)}, f32[4,12,256]{2,1,0:T(8,128)S(1)},...) while((s32[]{:T(128)}, f32[12,512]{1,0:T(8,128)S(1)}, ...), condition=%wide.region_2.3_spmd.clone, body=%wide.region_1.2_spmd.clone.sunk | while | flops 95716368 | bytes 3547396 | solution.py:45
  40.8 0.8 fusion.92
  42.8 0.5 fusion.93
  43.5 0.8 fusion.92
  45.0 0.5 convolution_bitcast_fusion.4
  45.5 0.5 fusion.93
  46.2 0.8 fusion.92
  47.7 0.5 convolution_bitcast_fusion.4
  48.2 0.5 fusion.93
  48.8 0.8 fusion.92
  50.4 0.5 convolution_bitcast_fusion.4
  50.9 0.5 fusion.93
  51.5 10.7 %psum.42 = f32[12,1024]{1,0:T(8,128)S(1)} all-reduce(f32[12,1024]{1,0:T(8,128)S(1)} %bitcast.169), channel_id=1, replica_groups=mesh['smp'=8,'var'=4] {'var'}, use_global_device_ids=true, to_apply=%region_3.4 | all-reduce | flops 12288 | bytes 98304 | tf_op jit(solution)/shard_map/psum | solution.py:70
  62.3 37.5 %all-reduce.1 = (f32[12,512]{1,0:T(8,128)S(1)}, f32[12,512]{1,0:T(8,128)S(1)}) all-reduce(f32[12,512]{1,0:T(8,128)S(1)} %get-tuple-element.82, f32[12,512]{1,0:T(8,128)S(1)} %get-tuple-element.81), channel_id=1, replica_groups=mesh['smp'=8,'var'=4] {'smp'}, use_global_device_ids=true, to_apply=%region_6.7 | all-reduce | flops 12288 | bytes 98304 | tf_op jit(solution)/shard_map/psum | solution.py:71
  99.9 10.8 %while.31 = (s32[]{:T(128)}, f32[12,512]{1,0:T(8,128)S(1)}, f32[12,512]{1,0:T(8,128)S(1)}, f32[4,12,256]{2,1,0:T(8,128)S(1)}, f32[4,12,256]{2,1,0:T(8,128)S(1)},...) while((s32[]{:T(128)}, f32[12,512]{1,0:T(8,128)S(1)}, ...), condition=%wide.region_8.9_spmd.clone, body=%wide.region_7.8_spmd.clone.sunk | while | flops 95716368 | bytes 3547396 | solution.py:45
  100.0 0.8 fusion.103
  102.1 0.5 fusion.104
  102.7 0.8 fusion.103
  104.8 0.5 fusion.104
  105.4 0.8 fusion.103
  107.5 0.5 fusion.104
  108.1 0.8 fusion.103
  110.2 0.5 fusion.104
  110.8 10.7 %psum.45 = f32[12,1024]{1,0:T(8,128)S(1)} all-reduce(f32[12,1024]{1,0:T(8,128)S(1)} %bitcast.170), channel_id=1, replica_groups=mesh['smp'=8,'var'=4] {'var'}, use_global_device_ids=true, to_apply=%region_9.10 | all-reduce | flops 12288 | bytes 98304 | tf_op jit(solution)/shard_map/psum | solution.py:70
  121.6 0.6 fusion.44
  122.2 33.4 %all-reduce = (f32[12,512]{1,0:T(8,128)S(1)}, f32[12,512]{1,0:T(8,128)S(1)}) all-reduce(f32[12,512]{1,0:T(8,128)S(1)} %get-tuple-element.85, f32[12,512]{1,0:T(8,128)S(1)} %get-tuple-element.84), channel_id=1, replica_groups=mesh['smp'=8,'var'=4] {'smp'}, use_global_device_ids=true, to_apply=%region_12.13 | all-reduce | flops 12288 | bytes 98304 | tf_op jit(solution)/shard_map/psum | solution.py:71
  155.6 0.7 fusion.47
  (83 shorter events, 9.8 us)
Async XLA Ops:
  0.6 0.8 copy-start.1
  7.7 0.7 copy-start.2
  39.8 0.9 copy-start
where the time goes:
time: 157 us; the launch traced here: 156 us
  blocking collectives  130 us (83%)
  matrix products  20.5 us (13%)
  local copies, waits for them, and re-layouts  2.55 us (2%)
  other arithmetic  2.3 us (1%)
    psum x2, blocking collectives, body(): sum_a, sum_b = lax.psum((part_a, part_b), 'smp')  70.9 us
    all_gather x1, blocking collectives, body(): freqs_block = lax.all_gather(own_freqs, 'smp', axis=1, tiled=True)  31.4 us
    psum x2, blocking collectives, body(): sum_q = lax.psum(part_q, 'var')  21.3 us
    dot_general x8, matrix products, expect_sums(): probs = jnp.einsum('kn,km->nm', shares_block, freqs_block, precision=HIGH)  6.22 us
    all_gather x1, blocking collectives, body(): shares_block = lax.all_gather(own_shares, 'var', axis=1, tiled=True)  6.22 us
    dot_general x8, matrix products, expect_sums(): jnp.einsum('km,nm->kn', 1.0 - freqs_block, ratio_ref, precision=HIGH)  4.22 us
    dot_general x8, matrix products, expect_sums(): jnp.einsum('km,nm->kn', freqs_block, ratio_alt, precision=HIGH)  4.14 us

commit v1 on v0

v1 whole, which is shorter than its diff:
```python
import functools

import jax
import jax.numpy as jnp
from jax import lax
from jax.experimental import pallas as pl
from jax.experimental.pallas import tpu as pltpu
from jax.sharding import PartitionSpec as P

ITERS = 2
CODES = 16
PAD = 16
F32 = jnp.float32
BF16 = jnp.bfloat16


def split(x, pieces):
    out = []
    for _ in range(pieces):
        piece = x.astype(BF16)
        out.append(piece)
        x = x - piece.astype(F32)
    return out


def dot(a, b):
    return jnp.dot(a, b, preferred_element_type=F32)


def em_kernel(
    nv, ns, dosage_hbm, shares_ref, freqs_ref, shares_out, freqs_out,
    dosage_ref, q_slots, f_slots, sq_send, sq_recv, sf_send, sf_recv,
    q_pad, f_pad, qt_ref, q2_ref, fs_ref, fta_ref, ftb_ref,
    load_sem, q_ss, q_rs, f_ss, f_rs, sq_ss, sq_rs, sf_ss, sf_rs,
):
    iv, js = lax.axis_index("var"), lax.axis_index("smp")
    pops, ws = shares_ref.shape
    wf = freqs_ref.shape[1]
    words, variants = dosage_ref.shape
    samples = words * CODES

    load = pltpu.make_async_copy(dosage_hbm, dosage_ref, load_sem)
    load.start()

    def var_peer(d):
        return lax.rem(iv + d, nv)

    def smp_peer(d):
        return lax.rem(js + d, ns)

    barrier = pltpu.get_barrier_semaphore()
    for d in range(1, ns):
        pl.semaphore_signal(barrier, inc=1, device_id=(smp_peer(d), iv), device_id_type=pl.DeviceIdType.MESH)
    for d in range(1, nv):
        pl.semaphore_signal(barrier, inc=1, device_id=(js, var_peer(d)), device_id_type=pl.DeviceIdType.MESH)

    q_own = shares_ref[...]
    q_own = q_own / jnp.sum(q_own, axis=0, keepdims=True)
    f_own = freqs_ref[...]
    q_pad[...] = jnp.zeros_like(q_pad)
    f_pad[...] = jnp.zeros_like(f_pad)
    q_slots[0, iv] = q_own
    f_slots[0, js] = f_own
    pl.semaphore_wait(barrier, ns - 1 + nv - 1)

    def copies_smp(src_of, dst, it, ss, rs):
        made = []
        for d in range(1, ns):
            to, frm = smp_peer(d), smp_peer(ns - d)
            send = pltpu.make_async_remote_copy(
                src_ref=src_of(to), dst_ref=dst.at[it, js], send_sem=ss.at[it, to], recv_sem=rs.at[it, js],
                device_id=(to, iv), device_id_type=pl.DeviceIdType.MESH)
            recv = pltpu.make_async_remote_copy(
                src_ref=src_of(to), dst_ref=dst.at[it, frm], send_sem=ss.at[it, to], recv_sem=rs.at[it, frm],
                device_id=(frm, iv), device_id_type=pl.DeviceIdType.MESH)
            made.append((send, recv))
        return made

    def copies_var(src_of, dst, it, ss, rs):
        made = []
        for d in range(1, nv):
            to, frm = var_peer(d), var_peer(nv - d)
            send = pltpu.make_async_remote_copy(
                src_ref=src_of(to), dst_ref=dst.at[it, iv], send_sem=ss.at[it, to], recv_sem=rs.at[it, iv],
                device_id=(js, to), device_id_type=pl.DeviceIdType.MESH)
            recv = pltpu.make_async_remote_copy(
                src_ref=src_of(to), dst_ref=dst.at[it, frm], send_sem=ss.at[it, to], recv_sem=rs.at[it, frm],
                device_id=(js, frm), device_id_type=pl.DeviceIdType.MESH)
            made.append((send, recv))
        return made

    def start(made):
        for send, _ in made:
            send.start()

    def arrive(made):
        for _, recv in made:
            recv.wait_recv()

    def sent(made):
        for send, _ in made:
            send.wait_send()

    sent_later = []
    for it in range(ITERS):
        last = it + 1 == ITERS
        f_copies = copies_smp(lambda to: f_slots.at[it, js], f_slots, it, f_ss, f_rs)
        q_copies = copies_var(lambda to: q_slots.at[it, iv], q_slots, it, q_ss, q_rs)
        start(f_copies)
        start(q_copies)
        sent_later += [f_copies, q_copies]

        arrive(q_copies)
        for v in range(nv):
            q_pad[0:pops, v * ws:(v + 1) * ws] = q_slots[it, v]
        qh, qm, ql = split(q_pad[...], 3)
        qs = jnp.concatenate([qh, qh, qm, qh, qm, ql, qm, ql], axis=0)
        qt_ref[...] = qs.astype(F32).T.astype(BF16)
        q2_ref[...] = jnp.concatenate([qh, qm], axis=0)
        if it == 0:
            load.wait()

        arrive(f_copies)
        for s in range(ns):
            f_pad[0:pops, s * wf:(s + 1) * wf] = f_slots[it, s]
        f_all = f_pad[...]
        fh, fm, fl = split(f_all, 3)
        gh, gm = split(1.0 - f_all, 2)
        fs_ref[...] = jnp.concatenate([fh, fm, fh, fl, fm, fh, fl, fm], axis=0)
        ft = jnp.concatenate([fh, fm, gh, gm, fh, fm, gh, gm], axis=0).astype(F32).T.astype(BF16)
        fta_ref[...] = ft[:, 0:2 * PAD]
        ftb_ref[...] = ft[:, 2 * PAD:4 * PAD]

        sum_a = jnp.zeros((2 * PAD, variants), F32)
        sum_b = jnp.zeros((2 * PAD, variants), F32)
        sq_parts = []
        rows = 256
        for b in range(samples // rows):
            here = slice(b * rows, (b + 1) * rows)
            packed = dosage_ref[b * rows // CODES:(b + 1) * rows // CODES, :]
            shape3 = (rows // CODES, CODES, variants)
            shifts = 2 * lax.broadcasted_iota(jnp.int32, shape3, 1)
            codes = jnp.bitwise_and(jnp.right_shift(jnp.broadcast_to(packed[:, None, :], shape3), shifts), 3)
            codes = codes.reshape(rows, variants)
            probs = dot(qt_ref[here, :], fs_ref[...])
            rest = 1.0 - probs
            inv = 1.0 / (probs * rest)
            live = codes < 3
            codes_f = codes.astype(F32)
            a = jnp.where(live, codes_f, 0.0) * (rest * inv)
            bb = jnp.where(live, 2.0 - codes_f, 0.0) * (probs * inv)
            ah, al = split(a, 2)
            bh, bl = split(bb, 2)
            q2 = q2_ref[:, here]
            sum_a = sum_a + dot(q2, ah) + dot(q2, al)
            sum_b = sum_b + dot(q2, bh) + dot(q2, bl)
            sq = (dot(ah, fta_ref[...]) + dot(al, fta_ref[...])) + (dot(bh, ftb_ref[...]) + dot(bl, ftb_ref[...]))
            sq_t = sq.T
            sq_parts.append(sq_t[0:PAD] + sq_t[PAD:2 * PAD])
        sum_a = (sum_a[0:PAD] + sum_a[PAD:2 * PAD])[0:pops]
        sum_b = (sum_b[0:PAD] + sum_b[PAD:2 * PAD])[0:pops]
        for s in range(ns):
            cut = slice(s * wf, (s + 1) * wf)
            sf_send[it, s] = jnp.concatenate([sum_a[:, cut], sum_b[:, cut]], axis=1)
        sf_copies = copies_smp(lambda to: sf_send.at[it, to], sf_recv, it, sf_ss, sf_rs)
        start(sf_copies)
        sum_q = jnp.concatenate(sq_parts, axis=1)[0:pops]
        for v in range(nv):
            sq_send[it, v] = sum_q[:, v * ws:(v + 1) * ws]
        sq_copies = copies_var(lambda to: sq_send.at[it, to], sq_recv, it, sq_ss, sq_rs)
        start(sq_copies)
        sent_later += [sf_copies, sq_copies]

        arrive(sq_copies)
        total = sq_send[it, iv]
        for d in range(1, nv):
            total = total + sq_recv[it, var_peer(d)]
        numer = q_own * total
        q_own = (numer + 0.5) / (jnp.sum(numer, axis=0, keepdims=True) + 0.5 * pops)
        if last:
            shares_out[...] = q_own
        else:
            q_slots[it + 1, iv] = q_own

        arrive(sf_copies)
        total = sf_send[it, js]
        for d in range(1, ns):
            total = total + sf_recv[it, smp_peer(d)]
        alt_part = f_own * total[:, 0:wf]
        ref_part = (1.0 - f_own) * total[:, wf:2 * wf]
        f_own = (alt_part + 0.5) / (alt_part + ref_part + 1.0)
        if last:
            freqs_out[...] = f_own
        else:
            f_slots[it + 1, js] = f_own

    for made in sent_later:
        sent(made)


def body(nv, ns, dosage, shares_init, freqs_init):
    pops, ws = shares_init.shape
    wf = freqs_init.shape[1]
    words, variants = dosage.shape
    samples = words * CODES
    vmem = pl.BlockSpec(memory_space=pltpu.VMEM)
    dma = pltpu.SemaphoreType.DMA
    return pl.pallas_call(
        functools.partial(em_kernel, nv, ns),
        out_shape=(
            jax.ShapeDtypeStruct((pops, ws), F32),
            jax.ShapeDtypeStruct((pops, wf), F32),
        ),
        in_specs=[pl.BlockSpec(memory_space=pl.ANY), vmem, vmem],
        out_specs=(vmem, vmem),
        scratch_shapes=[
            pltpu.VMEM((words, variants), jnp.int32),
            pltpu.VMEM((ITERS, nv, pops, ws), F32),
            pltpu.VMEM((ITERS, ns, pops, wf), F32),
            pltpu.VMEM((ITERS, nv, pops, ws), F32),
            pltpu.VMEM((ITERS, nv, pops, ws), F32),
            pltpu.VMEM((ITERS, ns, pops, 2 * wf), F32),
            pltpu.VMEM((ITERS, ns, pops, 2 * wf), F32),
            pltpu.VMEM((PAD, samples), F32),
            pltpu.VMEM((PAD, variants), F32),
            pltpu.VMEM((samples, 8 * PAD), BF16),
            pltpu.VMEM((2 * PAD, samples), BF16),
            pltpu.VMEM((8 * PAD, variants), BF16),
            pltpu.VMEM((variants, 2 * PAD), BF16),
            pltpu.VMEM((variants, 2 * PAD), BF16),
            dma,
            dma((ITERS, nv)), dma((ITERS, nv)),
            dma((ITERS, ns)), dma((ITERS, ns)),
            dma((ITERS, nv)), dma((ITERS, nv)),
            dma((ITERS, ns)), dma((ITERS, ns)),
        ],
        compiler_params=pltpu.CompilerParams(collective_id=0, has_side_effects=True),
        cost_estimate=pl.CostEstimate(flops=200000000, bytes_accessed=400000, transcendentals=1000000),
    )(dosage, shares_init, freqs_init)


def solution(mesh):
    placed = (P("smp", "var"), P(None, ("smp", "var")), P(None, ("var", "smp")))
    return jax.shard_map(
        functools.partial(body, mesh.shape["var"], mesh.shape["smp"]),
        mesh=mesh,
        in_specs=placed,
        out_specs=(P(None, ("smp", "var")), P(None, ("var", "smp"))),
        check_vma=False,
    )
```

time: 157 us -> 35.2 us (0.22)
  blocking collectives: 130 us -> 0 us
  Pallas kernels: 0 us -> 32.3 us
  matrix products: 20.5 us -> 0 us
  other arithmetic: 2.3 us -> 0 us
    psum x4 -> x0, blocking collectives: 92.2 us -> none  [the longest x2 70.9 us: body(): sum_a, sum_b = lax.psum((part_a, part_b), 'smp')]
    all_gather x2 -> x0, blocking collectives: 37.6 us -> none  [the longest x1 31.4 us: body(): freqs_block = lax.all_gather(own_freqs, 'smp', axis=1, tiled=True)]
    pallas_call x0 -> x1, Pallas kernels: none -> 32.3 us  [body(): pl.pallas_call(functools.partial(em_kernel, nv, ns), out_shape=(jax.Shape...]
    dot_general x40 -> x0, matrix products: 20.5 us -> none  [the longest x8 6.22 us: expect_sums(): probs = jnp.einsum('kn,km->nm', shares_block, freqs_block, precision=HIGH)]
where the time goes in v1:
time: 35.2 us; the launch traced here: 34.9 us
  Pallas kernels  32.3 us (92%)
  local copies, waits for them, and re-layouts  1.93 us (5%)
  between operations  0.65 us (2%)
    pallas_call x1, Pallas kernels, body(): pl.pallas_call(functools.partial(em_kernel, nv, ns), out_shape=(jax.Shape...  32.3 us
    unnamed x4, local copies, waits for them, and re-layouts  1.93 us

profile of v1, /device:TPU:0, one launch (start us, length us, event | category | flops | bytes accessed | tf_op | source)
XLA Modules:
  0.0 34.9 jit_solution(4993703871804251683)
XLA Ops:
  0.6 32.3 %shard_map.50 = (f32[12,256]{1,0:T(8,128)}, f32[12,64]{1,0:T(8,128)}) custom-call(s32[64,512]{1,0:T(8,128)} %dosage_hbm.1, f32[12,256]{1,0:T(8,128)} %shares_ref.1, f32[12,64]{1,0:T(8,128)} %freqs_ref.1), custom_call_target="tpu_custom_call" | custom-call | flops 200000000 | bytes 400000 | tf_op jit(solution)/shard_map/pallas_call | solution.py:208
  33.0 0.0 copy-start
  33.0 1.3 %copy.7 = f32[12,256]{1,0:T(8,128)} copy(f32[12,256]{1,0:T(8,128)} %get-tuple-element.4) | data formatting | bytes 24576
  34.3 0.0 copy-done
  34.3 0.6 %copy.8 = f32[12,64]{1,0:T(8,128)} copy(f32[12,64]{1,0:T(8,128)S(1)} %copy-done) | data formatting | bytes 6144
Async XLA Ops:
  33.0 1.3 %copy-start = (f32[12,64]{1,0:T(8,128)S(1)}, f32[12,64]{1,0:T(8,128)}, u32[]{:S(2)}) copy-start(f32[12,64]{1,0:T(8,128)} %get-tuple-element.5) | copy-start | bytes 9220

commit v2 on v1

v2 whole, which is shorter than its diff:
```python
import functools

import jax
import jax.numpy as jnp
from jax import lax
from jax.experimental import pallas as pl
from jax.experimental.pallas import tpu as pltpu
from jax.sharding import PartitionSpec as P

ITERS = 2
CODES = 16
PAD = 16
F32 = jnp.float32
BF16 = jnp.bfloat16


def split(x, pieces):
    out = []
    for _ in range(pieces):
        piece = x.astype(BF16)
        out.append(piece)
        x = x - piece.astype(F32)
    return out


def dot(a, b):
    return jnp.dot(a, b, preferred_element_type=F32)


def em_kernel(
    nv, ns, chunk, dosage_hbm, shares_hbm, freqs_hbm, shares_out, freqs_out,
    dosage_ref, shares_ref, freqs_ref, q_slots, f_slots, sq_send, sq_recv, sf_send, sf_recv,
    q_pad, f_pad, qt_ref, q2_ref, fs_ref, fta_ref, ftb_ref,
    load_sem, q_ss, q_rs, f_ss, f_rs, sq_ss, sq_rs, sf_ss, sf_rs,
):
    iv, js = lax.axis_index("var"), lax.axis_index("smp")
    pops, ws = shares_ref.shape
    wf = freqs_ref.shape[1]
    words, variants = dosage_ref.shape
    samples = words * CODES
    chunks = variants // chunk
    per = ns // chunks
    own_chunk, own_place = js // per, lax.rem(js, per)
    mesh_ids = pl.DeviceIdType.MESH

    def chunk_at(t):
        return lax.rem(own_chunk + t, chunks)

    def smp_peer(t, d):
        return chunk_at(t) * per + lax.rem(own_place + d, per)

    def var_peer(d):
        return lax.rem(iv + d, nv)

    smp_peers = [[smp_peer(t, d) for d in range(0 if t else 1, per)] for t in range(chunks)]
    all_smp = [p for t in reversed(range(chunks)) for p in smp_peers[t]]
    var_peers = [var_peer(d) for d in range(1, nv)]

    barrier = pltpu.get_barrier_semaphore()
    for p in all_smp:
        pl.semaphore_signal(barrier, inc=1, device_id=(p, iv), device_id_type=mesh_ids)
    for p in var_peers:
        pl.semaphore_signal(barrier, inc=1, device_id=(js, p), device_id_type=mesh_ids)

    load_q = pltpu.make_async_copy(shares_hbm, shares_ref, load_sem.at[0])
    load_f = pltpu.make_async_copy(freqs_hbm, f_slots.at[0, js], load_sem.at[1])
    load_f2 = pltpu.make_async_copy(freqs_hbm, freqs_ref, load_sem.at[2])
    load_d = pltpu.make_async_copy(dosage_hbm, dosage_ref, load_sem.at[3])
    load_q.start()
    load_f.start()
    load_f2.start()
    load_d.start()
    q_pad[...] = jnp.zeros_like(q_pad)
    f_pad[...] = jnp.zeros_like(f_pad)
    load_q.wait()
    q_own = shares_ref[...]
    q_own = q_own / jnp.sum(q_own, axis=0, keepdims=True)
    q_slots[0, iv] = q_own
    load_f.wait()
    load_f2.wait()
    f_own = freqs_ref[...]
    pl.semaphore_wait(barrier, ns - 1 + nv - 1)

    def smp_copy(src, dst, it, ss, rs, to, slot):
        return pltpu.make_async_remote_copy(
            src_ref=src, dst_ref=dst.at[it, slot], send_sem=ss.at[it, to], recv_sem=rs.at[it, slot],
            device_id=(to, iv), device_id_type=mesh_ids)

    def var_copy(src, dst, it, ss, rs, to, slot):
        return pltpu.make_async_remote_copy(
            src_ref=src, dst_ref=dst.at[it, slot], send_sem=ss.at[it, to], recv_sem=rs.at[it, slot],
            device_id=(js, to), device_id_type=mesh_ids)

    sent = []

    def start(copy):
        copy.start()
        sent.append(copy)

    rows = 256
    blocks = samples // rows
    for it in range(ITERS):
        last = it + 1 == ITERS
        if it == 0:
            for p in all_smp:
                start(smp_copy(f_slots.at[it, js], f_slots, it, f_ss, f_rs, p, js))
            for p in var_peers:
                start(var_copy(q_slots.at[it, iv], q_slots, it, q_ss, q_rs, p, iv))

        for p in var_peers:
            var_copy(q_slots.at[it, iv], q_slots, it, q_ss, q_rs, p, p).wait_recv()
        for v in range(nv):
            q_pad[0:pops, v * ws:(v + 1) * ws] = q_slots[it, v]
        qh, qm, ql = split(q_pad[...], 3)
        qs = jnp.concatenate([qh, qh, qm, qh, qm, ql, qm, ql], axis=0)
        qt_ref[...] = qs.astype(F32).T.astype(BF16)
        q2_ref[...] = jnp.concatenate([qh, qm], axis=0)
        if it == 0:
            load_d.wait()

        sq_acc = [jnp.zeros((rows, 2 * PAD), F32) for _ in range(blocks)]
        for t in range(chunks):
            c = chunk_at(t)
            for p in smp_peers[t]:
                smp_copy(f_slots.at[it, js], f_slots, it, f_ss, f_rs, p, p).wait_recv()
            for i in range(per):
                f_pad[0:pops, i * wf:(i + 1) * wf] = f_slots[it, c * per + i]
            f_all = f_pad[...]
            fh, fm, fl = split(f_all, 3)
            gh, gm = split(1.0 - f_all, 2)
            fs_ref[...] = jnp.concatenate([fh, fm, fh, fl, fm, fh, fl, fm], axis=0)
            ft = jnp.concatenate([fh, fm, gh, gm, fh, fm, gh, gm], axis=0).astype(F32).T.astype(BF16)
            fta_ref[...] = ft[:, 0:2 * PAD]
            ftb_ref[...] = ft[:, 2 * PAD:4 * PAD]

            sum_a = jnp.zeros((2 * PAD, chunk), F32)
            sum_b = jnp.zeros((2 * PAD, chunk), F32)
            lanes = pl.ds(pl.multiple_of(c * chunk, chunk), chunk)
            for b in range(blocks):
                here = slice(b * rows, (b + 1) * rows)
                packed = dosage_ref[b * rows // CODES:(b + 1) * rows // CODES, lanes]
                shape3 = (rows // CODES, CODES, chunk)
                shifts = 2 * lax.broadcasted_iota(jnp.int32, shape3, 1)
                codes = jnp.bitwise_and(jnp.right_shift(jnp.broadcast_to(packed[:, None, :], shape3), shifts), 3)
                codes = codes.reshape(rows, chunk)
                probs = dot(qt_ref[here, :], fs_ref[...])
                rest = 1.0 - probs
                inv = 1.0 / (probs * rest)
                live = codes < 3
                codes_f = codes.astype(F32)
                a = jnp.where(live, codes_f, 0.0) * (rest * inv)
                bb = jnp.where(live, 2.0 - codes_f, 0.0) * (probs * inv)
                ah, al = split(a, 2)
                bh, bl = split(bb, 2)
                q2 = q2_ref[:, here]
                sum_a = sum_a + dot(q2, ah) + dot(q2, al)
                sum_b = sum_b + dot(q2, bh) + dot(q2, bl)
                sq_acc[b] = sq_acc[b] + (dot(ah, fta_ref[...]) + dot(al, fta_ref[...])) + (
                    dot(bh, ftb_ref[...]) + dot(bl, ftb_ref[...]))
            sum_a = (sum_a[0:PAD] + sum_a[PAD:2 * PAD])[0:pops]
            sum_b = (sum_b[0:PAD] + sum_b[PAD:2 * PAD])[0:pops]
            for i in range(per):
                cut = slice(i * wf, (i + 1) * wf)
                sf_send[it, c * per + i] = jnp.concatenate([sum_a[:, cut], sum_b[:, cut]], axis=1)
            for p in smp_peers[t]:
                start(smp_copy(sf_send.at[it, p], sf_recv, it, sf_ss, sf_rs, p, js))

        sq_t = [x.T for x in sq_acc]
        sum_q = jnp.concatenate([x[0:PAD] + x[PAD:2 * PAD] for x in sq_t], axis=1)[0:pops]
        for v in range(nv):
            sq_send[it, v] = sum_q[:, v * ws:(v + 1) * ws]
        for p in var_peers:
            start(var_copy(sq_send.at[it, p], sq_recv, it, sq_ss, sq_rs, p, iv))

        total = sq_send[it, iv]
        for p in var_peers:
            var_copy(sq_send.at[it, p], sq_recv, it, sq_ss, sq_rs, p, p).wait_recv()
            total = total + sq_recv[it, p]
        numer = q_own * total
        q_own = (numer + 0.5) / (jnp.sum(numer, axis=0, keepdims=True) + 0.5 * pops)
        if last:
            shares_out[...] = q_own
        else:
            q_slots[it + 1, iv] = q_own
            for p in var_peers:
                start(var_copy(q_slots.at[it + 1, iv], q_slots, it + 1, q_ss, q_rs, p, iv))

        total = sf_send[it, js]
        for t in range(chunks):
            for p in smp_peers[t]:
                smp_copy(sf_send.at[it, p], sf_recv, it, sf_ss, sf_rs, p, p).wait_recv()
                total = total + sf_recv[it, p]
        alt_part = f_own * total[:, 0:wf]
        ref_part = (1.0 - f_own) * total[:, wf:2 * wf]
        f_own = (alt_part + 0.5) / (alt_part + ref_part + 1.0)
        if last:
            freqs_out[...] = f_own
        else:
            f_slots[it + 1, js] = f_own
            for p in all_smp:
                start(smp_copy(f_slots.at[it + 1, js], f_slots, it + 1, f_ss, f_rs, p, js))

    for copy in sent:
        copy.wait_send()


def hand_out(shares_ref, freqs_ref, shares_out, freqs_out):
    shares_out[...] = shares_ref[...]
    freqs_out[...] = freqs_ref[...]


def body(nv, ns, dosage, shares_init, freqs_init):
    pops, ws = shares_init.shape
    wf = freqs_init.shape[1]
    words, variants = dosage.shape
    samples = words * CODES
    chunk = variants // 2
    vmem = pl.BlockSpec(memory_space=pltpu.VMEM)
    hbm = pl.BlockSpec(memory_space=pl.ANY)
    dma = pltpu.SemaphoreType.DMA
    shapes = (jax.ShapeDtypeStruct((pops, ws), F32), jax.ShapeDtypeStruct((pops, wf), F32))
    shares, freqs = pl.pallas_call(
        functools.partial(em_kernel, nv, ns, chunk),
        out_shape=shapes,
        in_specs=[hbm, hbm, hbm],
        out_specs=(vmem, vmem),
        scratch_shapes=[
            pltpu.VMEM((words, variants), jnp.int32),
            pltpu.VMEM((pops, ws), F32),
            pltpu.VMEM((pops, wf), F32),
            pltpu.VMEM((ITERS, nv, pops, ws), F32),
            pltpu.VMEM((ITERS, ns, pops, wf), F32),
            pltpu.VMEM((ITERS, nv, pops, ws), F32),
            pltpu.VMEM((ITERS, nv, pops, ws), F32),
            pltpu.VMEM((ITERS, ns, pops, 2 * wf), F32),
            pltpu.VMEM((ITERS, ns, pops, 2 * wf), F32),
            pltpu.VMEM((PAD, samples), F32),
            pltpu.VMEM((PAD, chunk), F32),
            pltpu.VMEM((samples, 8 * PAD), BF16),
            pltpu.VMEM((2 * PAD, samples), BF16),
            pltpu.VMEM((8 * PAD, chunk), BF16),
            pltpu.VMEM((chunk, 2 * PAD), BF16),
            pltpu.VMEM((chunk, 2 * PAD), BF16),
            dma((4,)),
            dma((ITERS, nv)), dma((ITERS, nv)),
            dma((ITERS, ns)), dma((ITERS, ns)),
            dma((ITERS, nv)), dma((ITERS, nv)),
            dma((ITERS, ns)), dma((ITERS, ns)),
        ],
        compiler_params=pltpu.CompilerParams(collective_id=0, has_side_effects=True),
        cost_estimate=pl.CostEstimate(flops=200000000, bytes_accessed=400000, transcendentals=1000000),
    )(dosage, shares_init, freqs_init)
    return pl.pallas_call(
        hand_out, out_shape=shapes, in_specs=[vmem, vmem], out_specs=(vmem, vmem),
    )(shares, freqs)


def solution(mesh):
    placed = (P("smp", "var"), P(None, ("smp", "var")), P(None, ("var", "smp")))
    return jax.shard_map(
        functools.partial(body, mesh.shape["var"], mesh.shape["smp"]),
        mesh=mesh,
        in_specs=placed,
        out_specs=(P(None, ("smp", "var")), P(None, ("var", "smp"))),
        check_vma=False,
    )
```

time: 35.2 us -> 32.9 us (0.935)
  local copies, waits for them, and re-layouts: 1.93 us -> 0 us
    unnamed x4 -> x0, local copies, waits for them, and re-layouts: 1.93 us -> none
    pallas_call x1 -> x2, Pallas kernels: 32.3 us -> 32 us  [the longest x1 30.6 us: body(): pl.pallas_call(functools.partial(em_kernel, nv, ns, chunk), out_shape=sha...]
where the time goes in v2:
time: 32.9 us; the launch traced here: 32.6 us
  Pallas kernels  32 us (97%)
  between operations  0.64 us (2%)
    pallas_call x1, Pallas kernels, body(): pl.pallas_call(functools.partial(em_kernel, nv, ns, chunk), out_shape=sha...  30.6 us
    pallas_call x1, Pallas kernels, body(): pl.pallas_call(hand_out, out_shape=shapes, in_specs=[vmem, vmem], out_spe...  1.33 us

profile of v2, /device:TPU:0, one launch (start us, length us, event | category | flops | bytes accessed | tf_op | source)
XLA Modules:
  0.0 32.6 jit_solution(6727487163880301574)
XLA Ops:
  0.6 30.6 %shard_map.50 = (f32[12,256]{1,0:T(8,128)}, f32[12,64]{1,0:T(8,128)}) custom-call(s32[64,512]{1,0:T(8,128)} %dosage_hbm.1, f32[12,256]{1,0:T(8,128)} %shares_hbm.1, f32[12,64]{1,0:T(8,128)} %freqs_hbm.1), custom_call_target="tpu_custom_call" | custom-call | flops 200000000 | bytes 400000 | tf_op jit(solution)/shard_map/pallas_call | solution.py:222
  31.3 1.3 %shard_map.51 = (f32[12,256]{1,0:T(8,128)}, f32[12,64]{1,0:T(8,128)}) custom-call(f32[12,256]{1,0:T(8,128)} %get-tuple-element.4.shares_ref, f32[12,64]{1,0:T(8,128)} %get-tuple-element.5.freqs_ref), custom_call_target="tpu_custom_call" | custom-call | tf_op jit(solution)/shard_map/pallas_call | solution.py:253

commit v3 on v2

--- a/solution.py
+++ b/solution.py
@@ -30,7 +30,7 @@
 def em_kernel(
     nv, ns, chunk, dosage_hbm, shares_hbm, freqs_hbm, shares_out, freqs_out,
     dosage_ref, shares_ref, freqs_ref, q_slots, f_slots, sq_send, sq_recv, sf_send, sf_recv,
-    q_pad, f_pad, qt_ref, q2_ref, fs_ref, fta_ref, ftb_ref,
+    q_pad, f_pad, qt_ref, q2_ref, fs_ref, fgs_ref,
     load_sem, q_ss, q_rs, f_ss, f_rs, sq_ss, sq_rs, sf_ss, sf_rs,
 ):
     iv, js = lax.axis_index("var"), lax.axis_index("smp")
@@ -97,7 +97,7 @@
         copy.start()
         sent.append(copy)
 
-    rows = 256
+    rows = 512
     blocks = samples // rows
     for it in range(ITERS):
         last = it + 1 == ITERS
@@ -118,7 +118,7 @@
         if it == 0:
             load_d.wait()
 
-        sq_acc = [jnp.zeros((rows, 2 * PAD), F32) for _ in range(blocks)]
+        sq_acc = [jnp.zeros((2 * PAD, rows), F32) for _ in range(blocks)]
         for t in range(chunks):
             c = chunk_at(t)
             for p in smp_peers[t]:
@@ -129,9 +129,9 @@
             fh, fm, fl = split(f_all, 3)
             gh, gm = split(1.0 - f_all, 2)
             fs_ref[...] = jnp.concatenate([fh, fm, fh, fl, fm, fh, fl, fm], axis=0)
-            ft = jnp.concatenate([fh, fm, gh, gm, fh, fm, gh, gm], axis=0).astype(F32).T.astype(BF16)
-            fta_ref[...] = ft[:, 0:2 * PAD]
-            ftb_ref[...] = ft[:, 2 * PAD:4 * PAD]
+            fpair = jnp.concatenate([fh, fm], axis=0)
+            gpair = jnp.concatenate([gh, gm], axis=0)
+            fgs_ref[...] = jnp.concatenate([fpair, fpair, gpair, gpair], axis=1)
 
             sum_a = jnp.zeros((2 * PAD, chunk), F32)
             sum_b = jnp.zeros((2 * PAD, chunk), F32)
@@ -153,10 +153,12 @@
                 ah, al = split(a, 2)
                 bh, bl = split(bb, 2)
                 q2 = q2_ref[:, here]
-                sum_a = sum_a + dot(q2, ah) + dot(q2, al)
-                sum_b = sum_b + dot(q2, bh) + dot(q2, bl)
-                sq_acc[b] = sq_acc[b] + (dot(ah, fta_ref[...]) + dot(al, fta_ref[...])) + (
-                    dot(bh, ftb_ref[...]) + dot(bl, ftb_ref[...]))
+                q22 = jnp.concatenate([q2, q2], axis=1)
+                sum_a = sum_a + dot(q22, jnp.concatenate([ah, al], axis=0))
+                sum_b = sum_b + dot(q22, jnp.concatenate([bh, bl], axis=0))
+                sq_acc[b] = sq_acc[b] + lax.dot_general(
+                    fgs_ref[...], jnp.concatenate([ah, al, bh, bl], axis=1), (((1,), (1,)), ((), ())),
+                    preferred_element_type=F32)
             sum_a = (sum_a[0:PAD] + sum_a[PAD:2 * PAD])[0:pops]
             sum_b = (sum_b[0:PAD] + sum_b[PAD:2 * PAD])[0:pops]
             for i in range(per):
@@ -165,8 +167,7 @@
             for p in smp_peers[t]:
                 start(smp_copy(sf_send.at[it, p], sf_recv, it, sf_ss, sf_rs, p, js))
 
-        sq_t = [x.T for x in sq_acc]
-        sum_q = jnp.concatenate([x[0:PAD] + x[PAD:2 * PAD] for x in sq_t], axis=1)[0:pops]
+        sum_q = jnp.concatenate([x[0:PAD] + x[PAD:2 * PAD] for x in sq_acc], axis=1)[0:pops]
         for v in range(nv):
             sq_send[it, v] = sum_q[:, v * ws:(v + 1) * ws]
         for p in var_peers:
@@ -239,8 +240,7 @@
             pltpu.VMEM((samples, 8 * PAD), BF16),
             pltpu.VMEM((2 * PAD, samples), BF16),
             pltpu.VMEM((8 * PAD, chunk), BF16),
-            pltpu.VMEM((chunk, 2 * PAD), BF16),
-            pltpu.VMEM((chunk, 2 * PAD), BF16),
+            pltpu.VMEM((2 * PAD, 4 * chunk), BF16),
             dma((4,)),
             dma((ITERS, nv)), dma((ITERS, nv)),
             dma((ITERS, ns)), dma((ITERS, ns)),

time: 32.9 us -> 30.8 us (0.936)
  Pallas kernels: 32 us -> 29.8 us
    pallas_call x1, Pallas kernels: 30.6 us -> 28.5 us  [body(): pl.pallas_call(functools.partial(em_kernel, nv, ns, chunk), out_shape=sha...]
where the time goes in v3:
time: 30.8 us; the launch traced here: 30.4 us
  Pallas kernels  29.8 us (97%)
  between operations  0.64 us (2%)
    pallas_call x1, Pallas kernels, body(): pl.pallas_call(functools.partial(em_kernel, nv, ns, chunk), out_shape=sha...  28.5 us
    pallas_call x1, Pallas kernels, body(): pl.pallas_call(hand_out, out_shape=shapes, in_specs=[vmem, vmem], out_spe...  1.33 us

profile of v3, /device:TPU:0, one launch (start us, length us, event | category | flops | bytes accessed | tf_op | source)
XLA Modules:
  0.0 30.4 jit_solution(4379804515836836658)
XLA Ops:
  0.6 28.5 %shard_map.50 = (f32[12,256]{1,0:T(8,128)}, f32[12,64]{1,0:T(8,128)}) custom-call(s32[64,512]{1,0:T(8,128)} %dosage_hbm.1, f32[12,256]{1,0:T(8,128)} %shares_hbm.1, f32[12,64]{1,0:T(8,128)} %freqs_hbm.1), custom_call_target="tpu_custom_call" | custom-call | flops 200000000 | bytes 400000 | tf_op jit(solution)/shard_map/pallas_call | solution.py:223
  29.1 1.3 %shard_map.51 = (f32[12,256]{1,0:T(8,128)}, f32[12,64]{1,0:T(8,128)}) custom-call(f32[12,256]{1,0:T(8,128)} %get-tuple-element.4.shares_ref, f32[12,64]{1,0:T(8,128)} %get-tuple-element.5.freqs_ref), custom_call_target="tpu_custom_call" | custom-call | tf_op jit(solution)/shard_map/pallas_call | solution.py:253
